TPU v7x, 512 devices: a whole 4x8x8 slice. The times are simulated.
512 devices in a mesh: layer: 4 (over x_hi, core), row: 8 (over y), col: 16 (over z, x_lo).
Axes of the slice: x: 4 (x_hi: 2, x_lo: 2; x = x_hi * 2 + x_lo), y: 8, z: 8, core: 2. Of those that a mesh axis runs over, the one named last changes fastest.
Arguments:
- front_pivot: bfloat16 [512, 256, 256], P(('layer', 'row', 'col')), may hold values from -8 to 40, as said below
- front_border: bfloat16 [512, 512, 256], P(('layer', 'row', 'col')), may hold values from -0.625 to 0.625
- pivot_live: int32 [512], P(('layer', 'row', 'col')), may hold values from 128 to 256
- rows_live: int32 [512, 4], P(('layer', 'row', 'col')), may hold values from 64 to 128
- border_block: int32 [512, 4], P(('layer', 'row', 'col')), may hold values from 0 to 63, as said below
- row_map: int32 [512, 4, 128], P(('layer', 'row', 'col')), may hold values from 0 to 127, each once within a row
- separator: float32 [8, 1024, 4, 2048], P(None, 'row', None, 'col'), may hold values from -16 to 32, as said below
Outputs:
- factored: float32 [8, 1024, 4, 2048], P('layer', 'row', None, 'col')
Inputs may be any that keep to these rules, and one draw needn't show every extreme that they name: `front_pivot`: each leaf's pivot block is symmetric with a dominant diagonal. The separator's entries form a symmetric matrix that stays positive definite after the leaves' contributions are subtracted. `border_block`: the 4 blocks of one leaf are distinct. Among them no more than 1 leave the same remainder when divided by the number of grid rows, and no more than 1 the same remainder when divided by the number of grid columns; every leaf reaches both bounds. `row_map`: each group's entries are a permutation of 0 to 127. Pivot columns from pivot_live on are padding. Rows of a group from rows_live on are padding.
All inputs are finite; a program needn't handle non-finite values.
Results may differ from a plain program's by a relative error of at most 0.0003.
Values sent between devices are 32-bit elements; how exact they have to be, the bound alone decides.
A program may use at most 128 MiB of HBM per device.

v0:
```python
import jax
import jax.numpy as jnp
from jax import lax
from jax.sharding import PartitionSpec as P

highest = lax.Precision.HIGHEST


def broadcast(array, axis, root):
    return lax.dynamic_index_in_dim(lax.all_gather(array, axis), root, 0, keepdims=False)


def joined_along(blocks, dim):
    dims = list(blocks.shape[1:])
    dims[dim] *= blocks.shape[0]
    return jnp.moveaxis(blocks, 0, dim).reshape(dims)


def sent_to_all(array, axis):
    copies = jnp.broadcast_to(array, (lax.axis_size(axis), *array.shape))
    return lax.all_to_all(copies, axis, split_axis=0, concat_axis=0, tiled=True)


def gathered_copies(array, axis, dim):
    return joined_along(sent_to_all(array, axis), dim)


def split_up(array, dim, peers):
    before, after = (array.shape[:dim], array.shape[dim + 1 :])
    return jnp.moveaxis(array.reshape(*before, peers, -1, *after), dim, 0)


def edges_of(length, count):
    lap = length // count
    if lap >= 8:
        lap -= lap % 8
    return [lap * k for k in range(1, count)]


def cut_exchange(array, axis, pieces, split_dim, concat_dim):
    blocks = split_up(array, split_dim, lax.axis_size(axis))
    split_at = max(range(1, max(2, blocks.ndim - 1)), key=lambda d: blocks.shape[d])
    gathered = []
    for share in jnp.split(blocks, edges_of(blocks.shape[split_at], pieces), axis=split_at):
        if share.size:
            gathered.append(lax.all_to_all(share, axis, split_axis=0, concat_axis=0, tiled=True))
    return joined_along(jnp.concatenate(gathered, axis=split_at), concat_dim)


def sum_at_owner(array, axis, dim):
    blocks = split_up(array, dim, lax.axis_size(axis))
    arrived = lax.all_to_all(blocks, axis, split_axis=0, concat_axis=0, tiled=True)
    return arrived.sum(axis=0)


def leaf_tiles(pivot_front, border_front, pivot_count, row_counts, placement):
    pivot_width = pivot_front.shape[0]
    groups, block_size = placement.shape
    pivot_mask = (jnp.arange(pivot_width) < pivot_count).astype(jnp.float32)
    pivot_matrix = pivot_front.astype(jnp.float32) * pivot_mask[:, None] * pivot_mask[
        None, :
    ] + jnp.diag(1.0 - pivot_mask)
    factor = jnp.linalg.cholesky(pivot_matrix)
    row_mask = (
        (jnp.arange(block_size)[None, :] < row_counts[:, None])
        .astype(jnp.float32)
        .reshape(groups * block_size)
    )
    border = border_front.astype(jnp.float32) * row_mask[:, None] * pivot_mask[None, :]
    solved = jax.scipy.linalg.solve_triangular(factor, border.T, lower=True).T
    placing = (placement[:, None, :] == jnp.arange(block_size)[None, :, None]).astype(jnp.float32)
    placed = jnp.einsum(
        "gik,gkp->gip", placing, solved.reshape(groups, block_size, pivot_width), precision=highest
    )
    return jnp.einsum("gip,hjp->ghij", placed, placed, precision=highest)


def route_tiles(tiles, blocks, grid_rows, grid_cols, local_cols, col_slots, slots):
    groups = blocks.shape[0]
    block_size = tiles.shape[-1]
    row_home = blocks % grid_rows
    col_home = blocks % grid_cols
    before = jnp.arange(groups)[None, :] < jnp.arange(groups)[:, None]
    row_rank = jnp.sum(before & (row_home[None, :] == row_home[:, None]), axis=1)
    col_rank = jnp.sum(before & (col_home[None, :] == col_home[:, None]), axis=1)
    target = (
        (row_home[:, None] * grid_cols + col_home[None, :]) * slots
        + row_rank[:, None] * col_slots
        + col_rank[None, :]
    )
    labels = (blocks // grid_rows)[:, None] * local_cols + (blocks // grid_cols)[None, :]
    flat_target = target.reshape(groups * groups)
    outgoing = jnp.zeros((grid_rows * grid_cols * slots, block_size, block_size), jnp.float32)
    outgoing = outgoing.at[flat_target].set(tiles.reshape(groups * groups, block_size, block_size))
    markers = jnp.full((grid_rows * grid_cols * slots,), -1, jnp.int32)
    markers = markers.at[flat_target].set(labels.reshape(groups * groups))
    return (outgoing, markers)


def assemble_rows(received, markers, local_cols, count):
    block_size = received.shape[-1]
    total_slots = markers.shape[0]
    valid = markers >= 0
    row_hit = ((markers // local_cols)[:, None] == jnp.arange(count)[None, :]) & valid[:, None]
    col_hit = (markers % local_cols)[:, None] == jnp.arange(local_cols)[None, :]
    selector = (
        (row_hit[:, :, None] & col_hit[:, None, :])
        .astype(jnp.float32)
        .reshape(total_slots, count * local_cols)
    )
    summed = jnp.dot(
        selector.T, received.reshape(total_slots, block_size * block_size), precision=highest
    )
    return summed.reshape(count, local_cols, block_size, block_size).transpose(0, 2, 1, 3)


def factor_panels(matrix, row_offset):
    rows_here, block_size, local_cols = (matrix.shape[0], matrix.shape[1], matrix.shape[2])
    grid_rows = lax.axis_size("row")
    grid_cols = lax.axis_size("col")
    my_row = lax.axis_index("row")
    my_col = lax.axis_index("col")
    global_rows = (row_offset + jnp.arange(rows_here)) * grid_rows + my_row
    pick_rows = jnp.arange(local_cols) * (grid_cols // grid_rows) + my_col // grid_rows
    owner_col = 0 % grid_cols
    local_col = 0 // grid_cols
    owner_row = 0 % grid_rows
    owner_local = 0 // grid_rows
    column = matrix[:, :, local_col, :]
    candidate = column[owner_local % rows_here]
    diagonal = broadcast(
        candidate, ("layer", "row"), owner_local // rows_here * grid_rows + owner_row
    )
    pivot_factor = jnp.linalg.cholesky(diagonal)
    solved = jax.scipy.linalg.solve_triangular(
        pivot_factor, column.reshape(rows_here * block_size, block_size).T, lower=True
    ).T
    solved = solved.reshape(rows_here, block_size, block_size)
    below_pivot = (global_rows > 0)[:, None, None]
    at_pivot = (global_rows == 0)[:, None, None]
    panel_part = jnp.where(below_pivot, solved, jnp.where(at_pivot, pivot_factor[None, :, :], 0.0))
    own_rows = broadcast(panel_part, "col", owner_col)
    grid_panel = gathered_copies(own_rows, "layer", 0)
    crossing = broadcast(grid_panel[pick_rows], "row", my_col % grid_rows)
    update = jnp.einsum("aip,bjp->aibj", own_rows, crossing, precision=highest)
    matrix = matrix - update
    matrix = jnp.where(my_col == owner_col, matrix.at[:, :, local_col, :].set(own_rows), matrix)
    return matrix


def shards(front_pivot, front_border, pivot_live, rows_live, border_block, row_map, separator):
    tiles = leaf_tiles(front_pivot[0], front_border[0], pivot_live[0], rows_live[0], row_map[0])
    grid_rows = lax.axis_size("row")
    grid_cols = lax.axis_size("col")
    layers = lax.axis_size("layer")
    local_rows, block_size, local_cols = (
        separator.shape[0],
        separator.shape[1],
        separator.shape[2],
    )
    groups = border_block.shape[1]
    row_slots = -(-groups // grid_rows)
    col_slots = -(-groups // grid_cols)
    slots = row_slots * col_slots
    outgoing, markers = route_tiles(
        tiles, border_block[0], grid_rows, grid_cols, local_cols, col_slots, slots
    )
    received, arrived = (
        cut_exchange(outgoing, ("row", "col"), 2, 0, 0),
        cut_exchange(markers, ("row", "col"), 2, 0, 0),
    )
    share = local_rows // layers
    summed = sum_at_owner(
        assemble_rows(received, arrived, local_cols, share * lax.axis_size("layer")), "layer", 0
    )
    offset = lax.axis_index("layer") * share
    matrix = lax.dynamic_slice_in_dim(separator, offset, share, 0) - summed
    return factor_panels(matrix, offset)


def solution(mesh):
    placed = (
        P(("layer", "row", "col"), None, None),
        P(("layer", "row", "col"), None, None),
        P(("layer", "row", "col")),
        P(("layer", "row", "col"), None),
        P(("layer", "row", "col"), None),
        P(("layer", "row", "col"), None, None),
        P(None, "row", None, "col"),
    )
    return jax.shard_map(
        shards,
        mesh=mesh,
        in_specs=placed,
        out_specs=P("layer", "row", None, "col"),
        check_vma=False,
    )
```

profile of v0, /device:TPU:6, one launch (start us, length us, event | category | flops | bytes accessed | tf_op | source)
XLA Modules:
  0.0 644.4 jit_solution(10209225565275130856)
XLA Ops:
  6.5 0.8 fusion.33
  7.4 0.7 fusion.34
  9.2 0.7 copy.70
  9.9 19.0 %all-to-all-start = ((s32[128,1,1]{2,1,0:T(1,128)}), s32[128,1,1]{2,1,0:T(1,128)S(1)}, u32[]{:S(2)}, u32[]{:S(2)}) async-start(s32[128,1,1]{2,1,0:T(1,128)} %copy.70), calls=%async_computation | async-start | bytes 131072 | tf_op jit(solution)/shard_map/all_to_all | solution.py:46
  29.6 1.0 copy.71
  31.0 11.7 %cholesky.69 = f32[128,128]{1,0:T(8,128)S(1)} custom-call(f32[128,128]{1,0:T(8,128)S(1)} %cholesky.162), custom_call_target="Cholesky" | custom-call | tf_op jit(solution)/shard_map/jit(cholesky)/cholesky | solution.py:63
  42.8 9.8 %custom-call.22 = f32[1,128,128]{1,2,0:T(8,128)S(1)} custom-call(f32[1,128,128]{2,1,0:T(8,128)S(1)} %get-tuple-element.58), custom_call_target="InvertDiagBlocksLowerTriangular" | custom-call | tf_op jit(solution)/shard_map/jit(cholesky)/cholesky | solution.py:63
  53.3 11.7 %cholesky.142 = f32[128,128]{1,0:T(8,128)S(1)} custom-call(f32[128,128]{1,0:T(8,128)S(1)} %convolution_subtract_fusion.2), custom_call_target="Cholesky" | custom-call | tf_op jit(solution)/shard_map/jit(cholesky)/cholesky | solution.py:63
  65.1 0.7 compare_reduce_fusion.1
  67.2 4.0 while.3
  67.8 1.3 dynamic-slice.18
  69.8 1.3 dynamic-slice.18
  71.2 19.8 %custom-call.23 = f32[2,128,128]{1,2,0:T(8,128)S(1)} custom-call(f32[2,128,128]{2,1,0:T(8,128)S(1)} %get-tuple-element.24), custom_call_target="InvertDiagBlocksLowerTriangular" | custom-call | tf_op jit(solution)/shard_map/jit(_solve_triangular)/triangular_solve | solution.py:70
  93.4 2.0 convolution_bitcast_fusion
  95.4 1.6 copy.79
  97.0 4.3 broadcast_in_dim.47
  101.2 3.0 scatter_fusion
  104.2 8.5 %slice_bitcast_fusion.1 = (f32[128,1,64,128]{3,2,1,0:T(8,128)}, f32[128,1,64,128]{3,2,1,0:T(8,128)}) fusion(f32[128,1,128,128]{3,2,0,1:T(8,128)} %bitcast.159), kind=kLoop, calls=%fused_computation.9 | loop fusion | bytes 16777216 | tf_op jit(solution)/shard_map/split | solution.py:44
  112.7 110.7 %all_to_all.32 = f32[128,1,64,128]{3,2,1,0:T(8,128)} all-to-all(f32[128,1,64,128]{3,2,1,0:T(8,128)} %get-tuple-element.55), channel_id=1, replica_groups=mesh['layer'=4,'row'=8,'col'=16] {'row','col'}, dimensions={0} | all-to-all | bytes 8388608 | tf_op jit(solution)/shard_map/all_to_all | solution.py:46
  223.3 13.4 %all-to-all-start.2 = ((f32[128,1,64,128]{3,2,1,0:T(8,128)}), f32[128,1,64,128]{3,2,1,0:T(8,128)}, u32[]{:S(2)}, u32[]{:S(2)}) async-start(f32[128,1,64,128]{3,2,1,0:T(8,128)} %get-tuple-element.56), calls=%async_computation.2 | async-start | bytes 8388608 | tf_op jit(solution)/shard_map/all_to_all | solution.py:46
  236.7 2.4 reduce.20
  239.2 101.7 %all-to-all-done.2 = f32[128,1,64,128]{3,2,1,0:T(8,128)} async-done(((f32[128,1,64,128]{3,2,1,0:T(8,128)}), f32[128,1,64,128]{3,2,1,0:T(8,128)}, u32[]{:S(2)}, u32[]{:S(2)}) %all-to-all-start.2) | async-done | bytes 4194336 | tf_op jit(solution)/shard_map/all_to_all | solution.py:46
  340.9 7.8 %pad_maximum_fusion = f32[128,1,128,128]{3,2,1,0:T(8,128)} fusion(f32[128,1,64,128]{3,2,1,0:T(8,128)} %all-to-all-done.2, f32[128,1,64,128]{3,2,1,0:T(8,128)} %all_to_all.32), kind=kLoop, calls=%fused_computation.5 | loop fusion | flops 2097152 | bytes 16777216 | tf_op jit(solution)/shard_map/concatenate | solution.py:47
  348.7 9.3 %copy.101 = f32[128,1,128,128]{0,3,2,1:T(8,128)} copy(f32[128,1,128,128]{3,2,1,0:T(8,128)} %pad_maximum_fusion) | data formatting | bytes 16777216 | tf_op jit(solution)/shard_map/reshape;reshape | solution.py:112
  358.0 6.9 %fusion = f32[8,4,128,128]{3,0,2,1:T(8,128)S(1)} fusion(f32[128,1,128,128]{0,3,2,1:T(8,128)} %copy.101, pred[8,4,128,1]{2,1,0,3:T(4,128)(4,1)S(1)} %and_bitcast_fusion), kind=kOutput, calls=%fused_computation.6 | convolution fusion | flops 805306368 | bytes 10489856 | tf_op jit(solution)/shard_map/dot_general | solution.py:111
  364.9 2.4 copy.84
  367.3 4.8 all-to-all-start.3
  372.1 24.1 %all-to-all-done.3 = f32[4,2,128,4,128]{4,1,2,3,0:T(2,128)} async-done(((f32[4,2,128,4,128]{4,1,2,3,0:T(2,128)}), f32[4,2,128,4,128]{4,1,2,3,0:T(2,128)}, u32[]{:S(2)}, u32[]{:S(2)}) %all-to-all-start.3) | async-done | bytes 2097184 | tf_op jit(solution)/shard_map/all_to_all | solution.py:52
  396.2 3.6 reduce_sum.29
  399.8 1.1 copy_subtract_fusion
  401.9 75.5 %all-gather.7.cloned.1.call-done = f32[32,128,1,128]{3,1,2,0:T(8,128)} async-done(((f32[1,128,1,128]{3,1,2,0:T(8,128)}), f32[32,128,1,128]{3,1,2,0:T(8,128)}) %all-gather.7.cloned.1.call-update) | async-done | bytes 2097168 | tf_op jit(solution)/shard_map/all_gather | solution.py:10
  477.4 0.8 slice.119
  478.3 0.9 fusion.21
  479.2 11.7 %cholesky.154 = f32[128,128]{1,0:T(8,128)S(1)} custom-call(f32[128,128]{1,0:T(8,128)S(1)} %fusion.21), custom_call_target="Cholesky" | custom-call | tf_op jit(solution)/shard_map/jit(cholesky)/cholesky | solution.py:134
  490.9 0.6 compare_reduce_fusion
  491.6 0.7 select_bitcast_fusion
  492.2 9.8 %custom-call.24 = f32[1,128,128]{1,2,0:T(8,128)S(1)} custom-call(f32[1,128,128]{2,1,0:T(8,128)S(1)} %get-tuple-element.49), custom_call_target="InvertDiagBlocksLowerTriangular" | custom-call | tf_op jit(solution)/shard_map/jit(_solve_triangular)/triangular_solve | solution.py:135
  502.0 0.9 convolution_select_fusion
  503.0 73.0 %all-gather.9.cloned.1.call-done = f32[32,128,128]{2,1,0:T(8,128)} async-done(((f32[2,128,128]{2,1,0:T(8,128)}), f32[32,128,128]{2,1,0:T(8,128)}) %all-gather.9.cloned.1.call-update) | async-done | bytes 2097168 | tf_op jit(solution)/shard_map/all_gather | solution.py:10
  575.9 0.9 slice.120
  576.9 0.8 broadcast_in_dim.61
  577.7 5.3 all-to-all-start.4
  583.0 7.2 %all-to-all-done.4 = f32[4,2,128,128]{3,2,1,0:T(8,128)S(1)} async-done(((f32[4,2,128,128]{3,2,1,0:T(8,128)}), f32[4,2,128,128]{3,2,1,0:T(8,128)S(1)}, u32[]{:S(2)}, u32[]{:S(2)}) %all-to-all-start.4) | async-done | bytes 524320 | tf_op jit(solution)/shard_map/all_to_all | solution.py:21
  590.2 1.3 gather_fusion
  591.5 42.5 %all-gather.11.cloned.1.call-done = f32[32,128,128]{2,1,0:T(8,128)} async-done(((f32[4,128,128]{2,1,0:T(8,128)}), f32[32,128,128]{2,1,0:T(8,128)}) %all-gather.11.cloned.1.call-update) | async-done | bytes 2097168 | tf_op jit(solution)/shard_map/all_gather | solution.py:10
  634.0 1.6 convolution_subtract_fusion
  635.6 0.9 fusion.14
  636.5 1.1 copy.92
  (71 shorter events, 7.3 us)
Async XLA Ops:
  6.5 365.6 %copy-start = (f32[8,128,4,128]{3,2,1,0:T(4,128)S(1)}, f32[8,128,4,128]{3,2,1,0:T(4,128)}, u32[]{:S(2)}) copy-start(f32[8,128,4,128]{3,2,1,0:T(4,128)} %param.15) | copy-start | bytes 6291460
  6.5 84.5 %copy-start.1 = (bf16[1,512,256]{2,1,0:T(8,128)(2,1)S(1)}, bf16[1,512,256]{2,1,0:T(8,128)(2,1)}, u32[]{:S(2)}) copy-start(bf16[1,512,256]{2,1,0:T(8,128)(2,1)} %param.10) | copy-start | bytes 786436
  6.5 84.7 %copy-start.3 = (s32[1,4]{1,0:T(1,128)S(1)}, s32[1,4]{1,0:T(1,128)}, u32[]{:S(2)}) copy-start(s32[1,4]{1,0:T(1,128)} %param.12) | copy-start | bytes 52
  9.9 102.7 %all-to-all-start = ((s32[128,1,1]{2,1,0:T(1,128)}), s32[128,1,1]{2,1,0:T(1,128)S(1)}, u32[]{:S(2)}, u32[]{:S(2)}) async-start(s32[128,1,1]{2,1,0:T(1,128)} %copy.70), calls=%async_computation | async-start | bytes 131072 | tf_op jit(solution)/shard_map/all_to_all | solution.py:46
  67.0 25.9 %copy-start.2 = (s32[1,4,128]{2,1,0:T(4,128)S(1)}, s32[1,4,128]{2,1,0:T(4,128)}, u32[]{:S(2)}) copy-start(s32[1,4,128]{2,1,0:T(4,128)} %param.14) | copy-start | bytes 6148
  223.3 117.5 %all-to-all-start.2 = ((f32[128,1,64,128]{3,2,1,0:T(8,128)}), f32[128,1,64,128]{3,2,1,0:T(8,128)}, u32[]{:S(2)}, u32[]{:S(2)}) async-start(f32[128,1,64,128]{3,2,1,0:T(8,128)} %get-tuple-element.56), calls=%async_computation.2 | async-start | bytes 8388608 | tf_op jit(solution)/shard_map/all_to_all | solution.py:46
  367.3 28.9 %all-to-all-start.3 = ((f32[4,2,128,4,128]{4,1,2,3,0:T(2,128)}), f32[4,2,128,4,128]{4,1,2,3,0:T(2,128)}, u32[]{:S(2)}, u32[]{:S(2)}) async-start(f32[4,2,128,4,128]{4,1,2,3,0:T(2,128)} %copy.84), calls=%async_computation.3 | async-start | bytes 4194304 | tf_op jit(solution)/shard_map/all_to_all | solution.py:52
  372.1 105.3 %all-gather.7.cloned.1.call-start = ((), (), s32[]{:S(2)}) async-start(), calls=%async_computation.5 | async-start | bytes 2162688 | tf_op jit(solution)/shard_map/all_gather | solution.py:10
  401.6 174.4 %all-gather.9.cloned.1.call-start = ((), (), s32[]{:S(2)}) async-start(), calls=%async_computation.6 | async-start | bytes 2228224 | tf_op jit(solution)/shard_map/all_gather | solution.py:10
  577.7 12.5 %all-to-all-start.4 = ((f32[4,2,128,128]{3,2,1,0:T(8,128)}), f32[4,2,128,128]{3,2,1,0:T(8,128)S(1)}, u32[]{:S(2)}, u32[]{:S(2)}) async-start(f32[4,2,128,128]{3,2,1,0:T(8,128)} %broadcast_in_dim.61), calls=%async_computation.4 | async-start | bytes 1048576 | tf_op jit(solution)/shard_map/all_to_all | solution.py:21
  583.0 51.0 %all-gather.11.cloned.1.call-start = ((), (), s32[]{:S(2)}) async-start(), calls=%async_computation.7 | async-start | bytes 2359296 | tf_op jit(solution)/shard_map/all_gather | solution.py:10
Sparse Core Ops, SparseCore 0:
  401.7 75.6 all-gather.6
  503.1 72.7 all-gather.8
  591.6 42.3 all-gather.10
where the time goes:
time: 650 us; the launch traced here: 644 us
  waiting for transfers between devices  324 us (50%)
  blocking collectives  111 us (17%)
  other arithmetic  95.7 us (15%)
  starting transfers between devices  42.8 us (7%)
  local copies, waits for them, and re-layouts  42.1 us (6%)
  between operations  15.6 us (2%)
  matrix products  13.6 us (2%)
    all_gather x3, waiting for transfers between devices, broadcast(): lax.all_gather(array, axis)  191 us
    all_to_all x1, blocking collectives, cut_exchange(): lax.all_to_all(share, axis, split_axis=0, concat_axis=0, tiled=True)  111 us
    all_to_all x2, waiting for transfers between devices, cut_exchange(): lax.all_to_all(share, axis, split_axis=0, concat_axis=0, tiled=True)  102 us
    another operation x6, other arithmetic, leaf_tiles(): factor = jnp.linalg.cholesky(pivot_matrix)  34 us
    all_to_all x2, starting transfers between devices, cut_exchange(): lax.all_to_all(share, axis, split_axis=0, concat_axis=0, tiled=True)  32.4 us
    all_to_all x1, waiting for transfers between devices, sum_at_owner(): lax.all_to_all(blocks, axis, split_axis=0, concat_axis=0, tiled=True)  24.1 us
    another operation x3, other arithmetic, leaf_tiles(): solved = jax.scipy.linalg.solve_triangular(factor, border.T, lower=True).T  19.9 us
  transfers between devices with their start and end apart: 7, of which 6 were waited for; matrix products, arithmetic and copies ran while one was open for 13% of the time, Pallas kernels for 0%

commit v1 on v0

v1 whole, which is shorter than its diff:
```python
import jax
import jax.numpy as jnp
from jax import lax
from jax.experimental import pallas as pl
from jax.experimental.pallas import tpu as pltpu
from jax.sharding import PartitionSpec as P

f32 = jnp.float32
highest = lax.Precision.HIGHEST
MESH = pl.DeviceIdType.MESH
NB = 128
GROUP = 128
ROWS = 16
SHARE = 1088
VMEM = pl.BlockSpec(memory_space=pltpu.VMEM)
SMEM = pl.BlockSpec(memory_space=pltpu.SMEM)


def dot_nt(a, b):
    return lax.dot_general(
        a, b, (((1,), (1,)), ((), ())), precision=highest, preferred_element_type=f32
    )


def dot_nn(a, b):
    return lax.dot_general(
        a, b, (((1,), (0,)), ((), ())), precision=highest, preferred_element_type=f32
    )


def factor_and_inverse(matrix):
    count = NB // 8
    lane = lax.broadcasted_iota(jnp.int32, (8, NB), 1)
    sub = lax.broadcasted_iota(jnp.int32, (8, NB), 0)
    left = [matrix[8 * i : 8 * i + 8, :] for i in range(count)]
    right = [jnp.where(lane == sub + 8 * i, 1.0, 0.0).astype(f32) for i in range(count)]
    for k in range(NB):
        t, s = divmod(k, 8)
        left_row = left[t][s : s + 1, :]
        right_row = right[t][s : s + 1, :]
        inverse = 1.0 / left_row[:, k : k + 1]
        left_row = left_row * inverse
        right_row = right_row * inverse
        for i in range(t, count):
            column = jnp.broadcast_to(left[i][:, k : k + 1], (8, NB))
            if i == t:
                column = jnp.where(sub > s, column, 0.0)
            left[i] = left[i] - column * left_row
            right[i] = right[i] - column * right_row
    for i in range(count):
        on_diagonal = lane == sub + 8 * i
        pivots = jnp.sum(jnp.where(on_diagonal, left[i], 0.0), axis=1, keepdims=True)
        scale = 1.0 / jnp.sqrt(pivots)
        left[i] = jnp.where(lane >= sub + 8 * i, left[i] * scale, 0.0)
        right[i] = right[i] * scale
    return jnp.concatenate(left, axis=0), jnp.concatenate(right, axis=0)


def leaf_kernel(live_ref, rows_ref, block_ref, map_ref, pivot_ref, border_ref, sep_ref, out_ref):
    live = live_ref[0]
    row = lax.broadcasted_iota(jnp.int32, (256, 256), 0)
    col = lax.broadcasted_iota(jnp.int32, (256, 256), 1)
    front = jnp.where(
        (row < live) & (col < live),
        pivot_ref[...].astype(f32),
        jnp.where(row == col, 1.0, 0.0),
    )
    first = factor_and_inverse(front[:NB, :NB])[1]
    below = dot_nt(front[NB:, :NB], first)
    second = factor_and_inverse(front[NB:, NB:] - dot_nt(below, below))[1]

    blocks = [block_ref[g] for g in range(4)]
    ranks = []
    for g in range(4):
        rank = jnp.int32(0)
        for h in range(4):
            if h != g:
                rank = rank + jnp.where(blocks[h] > blocks[g], 1, 0)
        ranks.append(rank)
    border_row = lax.broadcasted_iota(jnp.int32, (NB, 256), 0)
    border_col = lax.broadcasted_iota(jnp.int32, (NB, 256), 1)
    home = lax.broadcasted_iota(jnp.int32, (NB, NB), 0)
    borders, placings, labels = [], [], []
    for s in range(4):
        g = jnp.int32(0)
        for h in range(1, 4):
            g = jnp.where(ranks[h] == s, h, g)
        labels.append(block_ref[g])
        rows = border_ref[pl.ds(pl.multiple_of(g * NB, NB), NB), :].astype(f32)
        keep = (border_row < rows_ref[g]) & (border_col < live)
        borders.append(jnp.where(keep, rows, 0.0))
        placings.append(jnp.where(map_ref[pl.ds(g, 1), :] == home, 1.0, 0.0).astype(f32))
    border = jnp.concatenate(borders, axis=0)
    solved_first = dot_nt(border[:, :NB], first)
    solved_second = dot_nt(border[:, NB:] - dot_nt(solved_first, below), second)
    solved = jnp.concatenate([solved_first, solved_second], axis=1)
    placed = jnp.concatenate(
        [dot_nn(placings[s], solved[s * NB : s * NB + NB]) for s in range(4)], axis=0
    )
    slot = 0
    for s in range(4):
        tiles = dot_nt(placed[s * NB : s * NB + NB], placed[s * NB :])
        for t in range(4 - s):
            out_ref[pl.ds(slot, NB, stride=ROWS), :] = tiles[:, t * NB : t * NB + NB]
            slot += 1
    for k in range(2):
        out_ref[pl.ds(10 + k, NB, stride=ROWS), :] = sep_ref[k]
    lane = lax.broadcasted_iota(jnp.int32, (NB, NB), 1)
    label_row = jnp.zeros((NB, NB), jnp.int32)
    for s in range(4):
        label_row = jnp.where(lane == s, labels[s], label_row)
    out_ref[pl.ds(12, NB, stride=ROWS), :] = label_row.astype(f32)
    for k in range(13, ROWS):
        out_ref[pl.ds(k, NB, stride=ROWS), :] = jnp.zeros((NB, NB), f32)


def exchange_kernel(src_ref, dst_ref, send_sem, recv_sem, own_sem):
    layer = lax.axis_index("layer")
    row = lax.axis_index("row")
    col = lax.axis_index("col")
    high, core, depth, low = layer // 2, layer % 2, col // 2, col % 2
    me = high * 64 + row * 8 + depth

    def peer(step):
        to_high = (high + step // 64) % 2
        to_row = (row + (step // 8) % 8) % 8
        to_depth = (depth + step % 8) % 8
        where_to = (to_high * 2 + core, to_row, to_depth * 2 + low)
        return to_high * 64 + to_row * 8 + to_depth, where_to

    barrier = pltpu.get_barrier_semaphore()

    def greet(step, carry):
        pl.semaphore_signal(barrier, inc=1, device_id=peer(step)[1], device_id_type=MESH)
        return carry

    lax.fori_loop(1, GROUP, greet, 0)
    own = pltpu.make_async_copy(src_ref.at[me], dst_ref.at[me], own_sem)
    own.start()
    pl.semaphore_wait(barrier, GROUP - 1)

    def send(index, carry):
        step = (index * 37) % GROUP
        target, where_to = peer(step)
        pltpu.make_async_remote_copy(
            src_ref=src_ref.at[target],
            dst_ref=dst_ref.at[me],
            send_sem=send_sem,
            recv_sem=recv_sem,
            device_id=where_to,
            device_id_type=MESH,
        ).start()
        return carry

    lax.fori_loop(1, GROUP, send, 0)
    own.wait()
    everything = pltpu.make_async_remote_copy(
        src_ref=src_ref.at[pl.ds(0, GROUP - 1)],
        dst_ref=dst_ref.at[pl.ds(0, GROUP - 1)],
        send_sem=send_sem,
        recv_sem=recv_sem,
        device_id=peer(1)[1],
        device_id_type=MESH,
    )
    everything.wait_send()
    everything.wait_recv()


def exchange(array, collective_id):
    return pl.pallas_call(
        exchange_kernel,
        out_shape=jax.ShapeDtypeStruct((GROUP, ROWS, NB), f32),
        in_specs=[VMEM],
        out_specs=VMEM,
        scratch_shapes=[pltpu.SemaphoreType.DMA] * 3,
        compiler_params=pltpu.CompilerParams(collective_id=collective_id, has_side_effects=True),
        name="exchange",
    )(array)


def collect_kernel(row_ref, col_ref, side_ref, got_ref, out_ref):
    def clear(i, carry):
        out_ref[pl.ds(pl.multiple_of(i * 64, 64), 64), :] = jnp.zeros((64, NB), f32)
        return carry

    lax.fori_loop(0, 4 * SHARE // 64, clear, 0)

    def add(leaf, carry):
        rows = [row_ref[leaf * 4 + g] for g in range(4)]
        cols = [col_ref[leaf * 4 + g] for g in range(4)]
        places, values = [], []
        slot = 0
        for s in range(4):
            for t in range(s, 4):
                value = got_ref[pl.ds(leaf * ROWS + slot, 1), :]
                slot += 1
                places.append(rows[s] + cols[t])
                values.append(value)
                if t > s:
                    places.append(rows[t] + cols[s])
                    values.append(value)
        before = [out_ref[pl.ds(place, 1), :] for place in places]
        for place, old, value in zip(places, before, values):
            out_ref[pl.ds(place, 1), :] = old + value
        return carry

    lax.fori_loop(0, GROUP, add, 0)
    for block in range(64):
        layer, kk, row = block // 16, (block // 8) % 2, block % 8
        high, core = layer // 2, layer % 2
        at = core * SHARE + high * 512 + row * 64 + kk * 4
        mine = jnp.where((side_ref[0] == 0) & (side_ref[1] == core), 1.0, 0.0)
        given = got_ref[pl.ds((high * 64 + row * 8) * ROWS + 10 + kk, 1), :]
        panel_row = out_ref[pl.ds(at, 1), :] - given * mine
        for q in range(4):
            out_ref[pl.ds(q * SHARE + 1024 + block, 1), :] = panel_row


def join_kernel(src_ref, out_ref, near, cross, passing, total, send_sem, recv_sem):
    layer = lax.axis_index("layer")
    row = lax.axis_index("row")
    col = lax.axis_index("col")
    core, low = layer % 2, col % 2
    twin = (layer + 1 - 2 * core, row, col)
    beside = (layer, row, col + 1 - 2 * low)
    barrier = pltpu.get_barrier_semaphore()
    for other in (twin, beside):
        pl.semaphore_signal(barrier, inc=1, device_id=other, device_id_type=MESH)
    pl.semaphore_wait(barrier, 2)

    def copy(src, dst, index, other):
        return pltpu.make_async_remote_copy(
            src_ref=src,
            dst_ref=dst,
            send_sem=send_sem.at[index],
            recv_sem=recv_sem.at[index],
            device_id=other,
            device_id_type=MESH,
        )

    onward = copy(src_ref.at[(1 - low) * 2 + 1 - core], near.at[0], 0, twin)
    kept = copy(src_ref.at[low * 2 + 1 - core], near.at[1], 1, twin)
    onward.start()
    kept.start()
    onward.wait()
    passing[...] = src_ref[(1 - low) * 2 + core] + near[0]
    across = copy(passing, cross, 2, beside)
    across.start()
    kept.wait()
    total[...] = src_ref[low * 2 + core] + near[1]
    across.wait()
    total[...] = total[...] + cross[...]

    def lay_out(d, carry):
        to_high, to_row, to_depth = d // 64, (d // 8) % 8, d % 8
        out_ref[d, 0:8, :] = total[pl.ds(pl.multiple_of(d * 8, 8), 8), :]
        for kk in range(2):
            block = (to_high * 2 + core) * 16 + kk * 8 + to_row
            out_ref[d, 8 + kk : 9 + kk, :] = total[pl.ds(1024 + block, 1), :]
        for kc in range(4):
            block = kc * 16 + to_depth * 2 + low
            out_ref[d, 10 + kc : 11 + kc, :] = total[pl.ds(1024 + block, 1), :]
        out_ref[d, 14:15, :] = total[1024:1025, :]
        out_ref[d, 15:16, :] = total[1024:1025, :]
        return carry

    lax.fori_loop(0, GROUP, lay_out, 0)


def panel_kernel(place_ref, got_ref, sep_ref, out_ref):
    layer, row, col = place_ref[0], place_ref[1], place_ref[2]

    def tile(slot):
        return got_ref[pl.ds(slot, NB, stride=ROWS), :]

    upper, inverse = factor_and_inverse(-tile(14))
    lower = upper.T
    owned, crossing = [], []
    for kk in range(2):
        at_pivot = (2 * layer + kk) * 8 + row == 0
        owned.append(jnp.where(at_pivot, lower, dot_nt(-tile(8 + kk), inverse)))
    for kc in range(4):
        at_pivot = kc * 16 + col == 0
        crossing.append(jnp.where(at_pivot, lower, dot_nt(-tile(10 + kc), inverse)))
    for kk in range(2):
        for kc in range(4):
            update = tile(kk * 4 + kc)
            above = (2 * layer + kk) * 8 + row < kc * 16 + col
            update = jnp.where(above, update.T, update)
            product = dot_nt(owned[kk], crossing[kc])
            result = sep_ref[kk, pl.ds(kc, NB, stride=4), :] - update - product
            if kc == 0:
                result = jnp.where(col == 0, owned[kk], result)
            out_ref[kk, pl.ds(kc, NB, stride=4), :] = result


def shards(front_pivot, front_border, pivot_live, rows_live, border_block, row_map, separator):
    layer = lax.axis_index("layer")
    row = lax.axis_index("row")
    col = lax.axis_index("col")
    own_sep = lax.dynamic_slice_in_dim(separator, layer * 2, 2, 0)
    outgoing = pl.pallas_call(
        leaf_kernel,
        out_shape=jax.ShapeDtypeStruct((GROUP * ROWS, NB), f32),
        in_specs=[SMEM] * 3 + [VMEM] * 4,
        out_specs=VMEM,
        name="leaf",
    )(
        pivot_live,
        rows_live[0],
        border_block[0],
        row_map[0],
        front_pivot[0],
        front_border[0],
        own_sep[:, :, 0, :],
    )
    got = exchange(outgoing.reshape(GROUP, ROWS, NB), 0)
    blocks = got[:, 12, :4].astype(jnp.int32)
    level = blocks // 16
    row_at = (level % 2) * SHARE + (level // 2) * 512 + (blocks % 8) * 64 + (blocks // 8 % 2) * 4
    col_at = (blocks % 2) * (2 * SHARE) + (blocks % 16 // 2) * 8 + level
    side = jnp.stack([col % 2, layer % 2]).astype(jnp.int32)
    gathered = pl.pallas_call(
        collect_kernel,
        out_shape=jax.ShapeDtypeStruct((4 * SHARE, NB), f32),
        in_specs=[SMEM] * 3 + [VMEM],
        out_specs=VMEM,
        name="collect",
    )(row_at.reshape(-1), col_at.reshape(-1), side, got.reshape(GROUP * ROWS, NB))
    laid_out = pl.pallas_call(
        join_kernel,
        out_shape=jax.ShapeDtypeStruct((GROUP, ROWS, NB), f32),
        in_specs=[VMEM],
        out_specs=VMEM,
        scratch_shapes=[
            pltpu.VMEM((2, SHARE, NB), f32),
            pltpu.VMEM((SHARE, NB), f32),
            pltpu.VMEM((SHARE, NB), f32),
            pltpu.VMEM((SHARE, NB), f32),
            pltpu.SemaphoreType.DMA((3,)),
            pltpu.SemaphoreType.DMA((3,)),
        ],
        compiler_params=pltpu.CompilerParams(collective_id=1, has_side_effects=True),
        name="join",
    )(gathered.reshape(4, SHARE, NB))
    final = exchange(laid_out, 2)
    place = jnp.stack([layer, row, col]).astype(jnp.int32)
    result = pl.pallas_call(
        panel_kernel,
        out_shape=jax.ShapeDtypeStruct((2, 4 * NB, NB), f32),
        in_specs=[SMEM, VMEM, VMEM],
        out_specs=VMEM,
        name="panel",
    )(place, final.reshape(GROUP * ROWS, NB), own_sep.reshape(2, 4 * NB, NB))
    return result.reshape(2, NB, 4, NB)


def solution(mesh):
    placed = (
        P(("layer", "row", "col"), None, None),
        P(("layer", "row", "col"), None, None),
        P(("layer", "row", "col")),
        P(("layer", "row", "col"), None),
        P(("layer", "row", "col"), None),
        P(("layer", "row", "col"), None, None),
        P(None, "row", None, "col"),
    )
    return jax.shard_map(
        shards,
        mesh=mesh,
        in_specs=placed,
        out_specs=P("layer", "row", None, "col"),
        check_vma=False,
    )
```

time: 650 us -> 167 us (0.26)
  waiting for transfers between devices: 324 us -> 0 us
  Pallas kernels: 0 us -> 161 us
  blocking collectives: 111 us -> 0 us
  other arithmetic: 95.7 us -> 3.13 us
  starting transfers between devices: 42.8 us -> 0 us
  local copies, waits for them, and re-layouts: 42.1 us -> 2.01 us
  between operations: 15.6 us -> 0.72 us
  matrix products: 13.6 us -> 0 us
    all_gather x3 -> x0, waiting for transfers between devices: 191 us -> none  [broadcast(): lax.all_gather(array, axis)]
    pallas_call x0 -> x6, Pallas kernels: none -> 161 us  [the longest x2 89.7 us: exchange(): pl.pallas_call(exchange_kernel, out_shape=jax.ShapeDtypeStruct((GROUP, RO...]
    all_to_all x4 -> x0, waiting for transfers between devices: 133 us -> none  [the longest x2 102 us: cut_exchange(): lax.all_to_all(share, axis, split_axis=0, concat_axis=0, tiled=True)]
    all_to_all x1 -> x0, blocking collectives: 111 us -> none  [cut_exchange(): lax.all_to_all(share, axis, split_axis=0, concat_axis=0, tiled=True)]
    another operation x14 -> x2, other arithmetic: 76.7 us -> 1.25 us  [the longest x1 0.64 us: shards(): side = jnp.stack([col % 2, layer % 2]).astype(jnp.int32)]
    all_to_all x4 -> x0, starting transfers between devices: 42.5 us -> none  [the longest x2 32.4 us: cut_exchange(): lax.all_to_all(share, axis, split_axis=0, concat_axis=0, tiled=True)]
    another operation x19 -> x0, local copies, waits for them, and re-layouts: 13.7 us -> none  [the longest x1 9.32 us: assemble_rows(): received.reshape(total_slots, block_size * block_size)]
    dot_general x4 -> x0, matrix products: 11 us -> none  [the longest x1 6.91 us: assemble_rows(): jnp.dot(selector.T, received.reshape(total_slots, block_size * block_size...]
  transfers between devices with their start and end apart: 7 -> 0, of which waited for: 6 -> 0; matrix products, arithmetic and copies ran while one was open for 13% -> 0% of each run, Pallas kernels for 0% -> 0%
where the time goes in v1:
time: 167 us
  Pallas kernels  161 us (96%)
  other arithmetic  3.13 us (2%)
  local copies, waits for them, and re-layouts  2.01 us (1%)
    pallas_call x2, Pallas kernels, exchange(): pl.pallas_call(exchange_kernel, out_shape=jax.ShapeDtypeStruct((GROUP, RO...  89.7 us
    pallas_call x1, Pallas kernels, shards(): pl.pallas_call(leaf_kernel, out_shape=jax.ShapeDtypeStruct((GROUP * ROWS,...  27 us
    pallas_call x1, Pallas kernels, shards(): pl.pallas_call(join_kernel, out_shape=jax.ShapeDtypeStruct((GROUP, ROWS,...  22.6 us
    pallas_call x1, Pallas kernels, shards(): pl.pallas_call(panel_kernel, out_shape=jax.ShapeDtypeStruct((2, 4 * NB, N...  15 us
    pallas_call x1, Pallas kernels, shards(): pl.pallas_call(collect_kernel, out_shape=jax.ShapeDtypeStruct((4 * SHARE,...  6.59 us

profile of v1, /device:TPU:6, one launch (start us, length us, event | category | flops | bytes accessed | tf_op | source)
XLA Modules:
  0.0 166.7 jit_solution(2772324393138435481)
XLA Ops:
  0.0 0.0 copy-start
  0.0 0.6 pad_add_fusion.place_ref
  1.3 0.3 copy-done
  1.6 0.7 constant_dynamic-slice_fusion
  2.3 27.0 %leaf.1 = f32[2048,128]{1,0:T(8,128)} custom-call(s32[1]{0:T(128)S(6)} %copy.14.live_ref, s32[4]{0:T(128)} %bitcast.28, s32[4]{0:T(128)} %bitcast.29, s32[4,128]{1,0:T(4,128)} %bitcast.27, bf16[256,256]{1,0:T(8,128)(2,1)} %bitcast.26, bf16[512,256]{1,0:T(8,128)(2,1)} %bitcast.25, f32[2,128,128]{2,1,0:T(8,128)} %bitcast.24), custom_call_target="tpu_custom_call" | custom-call | tf_op jit(solution)/shard_map/leaf/pallas_call | solution.py:302
  29.3 49.0 %exchange.2 = f32[128,16,128]{2,1,0:T(8,128)} custom-call(f32[128,16,128]{2,1,0:T(8,128)} %bitcast.22), custom_call_target="tpu_custom_call" | custom-call | tf_op jit(solution)/shard_map/exchange/pallas_call | solution.py:170
  78.3 1.3 convert_reduce_fusion
  79.6 0.1 convert_element_type.9
  79.7 0.6 fusion.10
  80.3 0.6 pad_add_fusion.1.side_ref
  80.9 6.6 %collect.1 = f32[4352,128]{1,0:T(8,128)} custom-call(s32[512]{0:T(512)} %get-tuple-element.6.row_ref, s32[512]{0:T(512)} %get-tuple-element.5.col_ref, s32[2]{0:T(128)} %pad_add_fusion.1.side_ref, f32[2048,128]{1,0:T(8,128)} %bitcast.20), custom_call_target="tpu_custom_call" | custom-call | tf_op jit(solution)/shard_map/collect/pallas_call | solution.py:323
  87.5 22.6 %join.1.src_ref = f32[128,16,128]{2,1,0:T(8,128)} custom-call(f32[4,1088,128]{2,1,0:T(8,128)} %bitcast.19), custom_call_target="tpu_custom_call" | custom-call | tf_op jit(solution)/shard_map/join/pallas_call | solution.py:330
  110.1 40.7 %exchange.3 = f32[128,16,128]{2,1,0:T(8,128)} custom-call(f32[128,16,128]{2,1,0:T(8,128)} %join.1.src_ref), custom_call_target="tpu_custom_call" | custom-call | tf_op jit(solution)/shard_map/exchange/pallas_call | solution.py:170
  150.9 0.9 constant_dynamic-slice_fusion.1
  151.7 15.0 %panel.1 = f32[2,512,128]{2,1,0:T(8,128)} custom-call(s32[3]{0:T(128)} %pad_add_fusion.place_ref, f32[2048,128]{1,0:T(8,128)} %bitcast.21, f32[2,512,128]{2,1,0:T(8,128)} %bitcast.23), custom_call_target="tpu_custom_call" | custom-call | tf_op jit(solution)/shard_map/panel/pallas_call | solution.py:348
Async XLA Ops:
  0.0 1.6 copy-start

commit v2 on v1

v2 whole, which is shorter than its diff:
```python
import jax
import jax.numpy as jnp
from jax import lax
from jax.experimental import pallas as pl
from jax.experimental.pallas import tpu as pltpu
from jax.sharding import PartitionSpec as P

f32 = jnp.float32
highest = lax.Precision.HIGHEST
MESH = pl.DeviceIdType.MESH
NB = 128
GROUP = 128
ROWS = 16
VMEM = pl.BlockSpec(memory_space=pltpu.VMEM)
SMEM = pl.BlockSpec(memory_space=pltpu.SMEM)


def dot_nt(a, b):
    return lax.dot_general(
        a, b, (((1,), (1,)), ((), ())), precision=highest, preferred_element_type=f32
    )


def dot_nn(a, b):
    return lax.dot_general(
        a, b, (((1,), (0,)), ((), ())), precision=highest, preferred_element_type=f32
    )


def factor_and_inverse(matrix):
    count = NB // 8
    lane = lax.broadcasted_iota(jnp.int32, (8, NB), 1)
    sub = lax.broadcasted_iota(jnp.int32, (8, NB), 0)

    def spread(block, s):
        return jnp.broadcast_to(block[s : s + 1, :], (8, NB))

    left = [matrix[8 * i : 8 * i + 8, :] for i in range(count)]
    right = [jnp.where(lane == sub + 8 * i, 1.0, 0.0).astype(f32) for i in range(count)]
    upper, inverse = [], []
    for t in range(count):
        columns = [
            [jnp.broadcast_to(left[i][:, 8 * t + s : 8 * t + s + 1], (8, NB)) for s in range(8)]
            for i in range(t, count)
        ]
        own = list(columns[0])
        rows, units = left[t], right[t]
        upper_rows, unit_rows, pivots = rows, units, own[0]
        for s in range(8):
            here = sub == s
            pivot = spread(own[s], s)
            scale = 1.0 / pivot
            row, unit = spread(rows, s), spread(units, s)
            upper_rows = jnp.where(here, row, upper_rows)
            unit_rows = jnp.where(here, unit, unit_rows)
            pivots = jnp.where(here, pivot, pivots)
            for j in range(s + 1, 8):
                ahead = spread(own[j], s) * scale
                own[j] = jnp.where(here, ahead, own[j] - own[s] * ahead)
            row, unit = row * scale, unit * scale
            rows = jnp.where(here, row, rows - own[s] * row)
            units = jnp.where(here, unit, units - own[s] * unit)
        for i in range(t + 1, count):
            for s in range(8):
                column = columns[i - t][s]
                left[i] = left[i] - column * spread(rows, s)
                right[i] = right[i] - column * spread(units, s)
        root = 1.0 / jnp.sqrt(pivots)
        upper.append(jnp.where(lane >= sub + 8 * t, upper_rows * root, 0.0))
        inverse.append(unit_rows * root)
    return jnp.concatenate(upper, axis=0), jnp.concatenate(inverse, axis=0)


class Peers:
    def __init__(self):
        self.layer = lax.axis_index("layer")
        self.row = lax.axis_index("row")
        self.col = lax.axis_index("col")
        self.high, self.core = self.layer // 2, lax.rem(self.layer, 2)
        self.depth, self.low = self.col // 2, lax.rem(self.col, 2)
        self.depths = [lax.rem(self.depth + dz, 8) for dz in range(8)]
        self.me = self.high * 64 + self.row * 8 + self.depth

    def at(self, dx, dy, dz):
        to_high = self.high if dx == 0 else 1 - self.high
        to_row = lax.rem(self.row + dy, 8)
        to_depth = self.depths[dz]
        place = (to_high * 2 + self.core, to_row, to_depth * 2 + self.low)
        return to_high * 64 + to_row * 8 + to_depth, place

    def visit(self, act, steps=range(8)):
        for dz in steps:
            if dz:
                act(*self.at(0, 0, dz))

        def near(dy, carry):
            for dz in steps:
                act(*self.at(0, dy, dz))
            return carry

        def far(dy, carry):
            for dz in steps:
                act(*self.at(1, dy, dz))
            return carry

        lax.fori_loop(1, 8, near, 0)
        lax.fori_loop(0, 8, far, 0)


def remote(src, dst, send_sem, recv_sem, place):
    return pltpu.make_async_remote_copy(
        src_ref=src,
        dst_ref=dst,
        send_sem=send_sem,
        recv_sem=recv_sem,
        device_id=place,
        device_id_type=MESH,
    )


def leaf_kernel(
    live_ref, rows_ref, block_ref, map_ref, pivot_ref, border_ref, sep_ref,
    got_ref, side_ref, out, early, send_sem, recv_sem, own_sem,
):
    peers = Peers()
    barrier = pltpu.get_barrier_semaphore()

    def greet(target, place):
        pl.semaphore_signal(barrier, inc=1, device_id=place, device_id_type=MESH)

    peers.visit(greet)

    blocks = [block_ref[g] for g in range(4)]
    ranks = []
    for g in range(4):
        rank = jnp.int32(0)
        for h in range(4):
            if h != g:
                rank = rank + jnp.where(blocks[h] > blocks[g], 1, 0)
        ranks.append(rank)
    order, labels = [], []
    for s in range(4):
        g, b = jnp.int32(0), blocks[0]
        for h in range(1, 4):
            g = jnp.where(ranks[h] == s, h, g)
            b = jnp.where(ranks[h] == s, blocks[h], b)
        order.append(g)
        labels.append(b)
    lane = lax.broadcasted_iota(jnp.int32, (NB, NB), 1)
    where_row = jnp.zeros((NB, NB), jnp.int32)
    for s in range(4):
        b = labels[s]
        level = b // 16
        row_at = (level % 2) * 1024 + (level // 2) * 512 + (b % 8) * 64 + (b // 8 % 2) * 4
        col_at = (b % 2) * 2048 + (b % 16 // 2) * 8 + level
        where_row = jnp.where(lane == s, row_at, where_row)
        where_row = jnp.where(lane == 4 + s, col_at, where_row)
    early_rows = early.reshape(GROUP * 8, NB)
    for k in range(2):
        early_rows[pl.ds(k, NB, stride=8), :] = sep_ref[k]
    early_rows[pl.ds(2, NB, stride=8), :] = where_row.astype(f32)

    live = live_ref[0]
    row = lax.broadcasted_iota(jnp.int32, (256, 256), 0)
    col = lax.broadcasted_iota(jnp.int32, (256, 256), 1)
    front = jnp.where(
        (row < live) & (col < live),
        pivot_ref[...].astype(f32),
        jnp.where(row == col, 1.0, 0.0),
    )
    first = factor_and_inverse(front[:NB, :NB])[1]

    pl.semaphore_wait(barrier, GROUP - 1)
    own_side = pltpu.make_async_copy(
        early.at[peers.me, pl.ds(0, 3)], side_ref.at[peers.me, pl.ds(0, 3)], own_sem.at[0]
    )
    own_side.start()

    def send_early(target, place):
        remote(
            early.at[target, pl.ds(0, 3)],
            side_ref.at[peers.me, pl.ds(0, 3)],
            send_sem.at[0],
            recv_sem.at[0],
            place,
        ).start()

    peers.visit(send_early)

    below = dot_nt(front[NB:, :NB], first)
    second = factor_and_inverse(front[NB:, NB:] - dot_nt(below, below))[1]
    border_row = lax.broadcasted_iota(jnp.int32, (NB, 256), 0)
    border_col = lax.broadcasted_iota(jnp.int32, (NB, 256), 1)
    home = lax.broadcasted_iota(jnp.int32, (NB, NB), 0)
    borders, placings = [], []
    for g in range(4):
        rows = border_ref[g * NB : g * NB + NB, :].astype(f32)
        keep = (border_row < rows_ref[g]) & (border_col < live)
        borders.append(jnp.where(keep, rows, 0.0))
        placings.append(jnp.where(map_ref[g : g + 1, :] == home, 1.0, 0.0).astype(f32))
    border = jnp.concatenate(borders, axis=0)
    solved_first = dot_nt(border[:, :NB], first)
    solved_second = dot_nt(border[:, NB:] - dot_nt(solved_first, below), second)
    solved = jnp.concatenate([solved_first, solved_second], axis=1)
    by_group = [dot_nn(placings[g], solved[g * NB : g * NB + NB]) for g in range(4)]
    in_order = []
    for s in range(4):
        chosen = by_group[0]
        for g in range(1, 4):
            chosen = jnp.where(order[s] == g, by_group[g], chosen)
        in_order.append(chosen)
    placed = jnp.concatenate(in_order, axis=0)
    out_rows = out.reshape(GROUP * ROWS, NB)
    slot = 0
    for s in range(4):
        tiles = dot_nt(placed[s * NB : s * NB + NB], placed[s * NB :])
        for t in range(4 - s):
            out_rows[pl.ds(slot, NB, stride=ROWS), :] = tiles[:, t * NB : t * NB + NB]
            slot += 1
    own_tiles = pltpu.make_async_copy(
        out.at[peers.me, pl.ds(0, 10)], got_ref.at[peers.me, pl.ds(0, 10)], own_sem.at[1]
    )
    own_tiles.start()

    def send_tiles(target, place):
        remote(
            out.at[target, pl.ds(0, 10)],
            got_ref.at[peers.me, pl.ds(0, 10)],
            send_sem.at[1],
            recv_sem.at[1],
            place,
        ).start()

    peers.visit(send_tiles)
    own_side.wait()
    own_tiles.wait()
    for index, src, dst, size in ((0, early, side_ref, 3), (1, out, got_ref, 10)):
        everything = remote(
            src.at[pl.ds(0, GROUP - 1), pl.ds(0, size)],
            dst.at[pl.ds(0, GROUP - 1), pl.ds(0, size)],
            send_sem.at[index],
            recv_sem.at[index],
            peers.at(0, 0, 1)[1],
        )
        everything.wait_send()
        everything.wait_recv()


def collect_kernel(where_ref, got_ref, side_ref, out_ref, panel_ref):
    core_here = lax.rem(lax.axis_index("layer"), 2)
    low = lax.rem(lax.axis_index("col"), 2)

    def clear(i, carry):
        out_ref[pl.ds(pl.multiple_of(i * 128, 128), 128), :] = jnp.zeros((128, NB), f32)
        return carry

    lax.fori_loop(0, 32, clear, 0)

    def add(leaf, carry):
        rows = [where_ref[leaf * 8 + g] for g in range(4)]
        cols = [where_ref[leaf * 8 + 4 + g] for g in range(4)]
        places, values = [], []
        slot = 0
        for s in range(4):
            for t in range(s, 4):
                value = got_ref[pl.ds(leaf * ROWS + slot, 1), :]
                slot += 1
                places.append(rows[s] + cols[t])
                values.append(value)
                if t > s:
                    places.append(rows[t] + cols[s])
                    values.append(value)
        before = [out_ref[pl.ds(place, 1), :] for place in places]
        for place, old, value in zip(places, before, values):
            out_ref[pl.ds(place, 1), :] = old + value
        return carry

    lax.fori_loop(0, GROUP, add, 0)
    for block in range(64):
        layer, kk, row = block // 16, (block // 8) % 2, block % 8
        high, core = layer // 2, layer % 2
        at = core * 1024 + high * 512 + row * 64 + kk * 4
        mine = jnp.where((low == 0) & (core_here == core), 1.0, 0.0)
        given = side_ref[pl.ds((high * 64 + row * 8) * 8 + kk, 1), :]
        panel_ref[pl.ds(block, 1), :] = out_ref[pl.ds(at, 1), :] - given * mine


def finish_kernel(
    src_ref, panel_ref, sep_ref, out_ref, near, cross, passing, total, joined, others, fan,
    got, extra, twin_send, twin_recv, cross_send, cross_recv, panel_send, panel_recv,
    send_sem, recv_sem, own_sem,
):
    peers = Peers()
    layer, row, col = peers.layer, peers.row, peers.col
    core, low, me = peers.core, peers.low, peers.me
    twin = (layer + 1 - 2 * core, row, col)
    beside = (layer, row, col + 1 - 2 * low)
    opposite = (layer + 1 - 2 * core, row, col + 1 - 2 * low)
    barrier = pltpu.get_barrier_semaphore()

    def greet(target, place):
        pl.semaphore_signal(barrier, inc=1, device_id=place, device_id_type=MESH)

    for place in (twin, beside, opposite):
        greet(0, place)
    peers.visit(greet)
    pl.semaphore_wait(barrier, GROUP + 2)

    panels = []
    for index, place in enumerate((twin, beside, opposite)):
        panels.append(
            remote(panel_ref, others.at[index], panel_send.at[index], panel_recv.at[index], place)
        )
    onward = remote(
        src_ref.at[(1 - low) * 2 + 1 - core], near.at[0], twin_send.at[0], twin_recv.at[0], twin
    )
    kept = remote(
        src_ref.at[low * 2 + 1 - core], near.at[1], twin_send.at[1], twin_recv.at[1], twin
    )
    for copy in (*panels, onward, kept):
        copy.start()

    onward.wait()
    across = []
    for dz in range(8):
        piece = pl.ds(pl.multiple_of(peers.depths[dz] * 8, 8), 8)
        passing[:, piece, :] = src_ref[(1 - low) * 2 + core, :, piece, :] + near[0, :, piece, :]
        across.append(
            remote(
                passing.at[:, piece],
                cross.at[:, piece],
                cross_send.at[dz],
                cross_recv.at[dz],
                beside,
            )
        )
        if dz < 2:
            across[dz].start()

    for copy in panels:
        copy.wait()
    joined[...] = panel_ref[...] + others[0] + others[1] + others[2]

    def lay_out(d, carry):
        to_high, to_row, to_depth = d // 64, lax.rem(d // 8, 8), lax.rem(d, 8)
        for kk in range(2):
            block = (to_high * 2 + core) * 16 + kk * 8 + to_row
            fan[d, kk : kk + 1, :] = joined[pl.ds(block, 1), :]
        for kc in range(4):
            block = kc * 16 + to_depth * 2 + low
            fan[d, 2 + kc : 3 + kc, :] = joined[pl.ds(block, 1), :]
        fan[d, 6:7, :] = joined[0:1, :]
        return carry

    lax.fori_loop(0, GROUP, lay_out, 0)
    own_extra = pltpu.make_async_copy(
        fan.at[me, pl.ds(0, 7)], extra.at[me, pl.ds(0, 7)], own_sem.at[0]
    )
    own_extra.start()

    def send_extra(target, place):
        remote(
            fan.at[target, pl.ds(0, 7)],
            extra.at[me, pl.ds(0, 7)],
            send_sem.at[0],
            recv_sem.at[0],
            place,
        ).start()

    peers.visit(send_extra)
    for dz in range(2, 8):
        across[dz].start()
    kept.wait()
    own_rows = None
    for dz in range(8):
        piece = pl.ds(pl.multiple_of(peers.depths[dz] * 8, 8), 8)
        across[dz].wait()
        total[:, piece, :] = (
            src_ref[low * 2 + core, :, piece, :] + near[1, :, piece, :] + cross[:, piece, :]
        )
        if dz == 0:
            own_rows = pltpu.make_async_copy(
                total.at[peers.high * 8 + row, piece], got.at[me], own_sem.at[1]
            )
            own_rows.start()

        def send_rows(target, place, piece=piece):
            remote(
                total.at[target // 8, piece], got.at[me], send_sem.at[1], recv_sem.at[1], place
            ).start()

        peers.visit(send_rows, (dz,))

    def arrived(index, src, dst, size):
        everything = remote(
            src.at[pl.ds(0, GROUP - 1), pl.ds(0, size)],
            dst.at[pl.ds(0, GROUP - 1), pl.ds(0, size)],
            send_sem.at[index],
            recv_sem.at[index],
            peers.at(0, 0, 1)[1],
        )
        everything.wait_send()
        everything.wait_recv()

    own_extra.wait()
    arrived(0, fan, extra, 7)
    extra_rows = extra.reshape(GROUP * 8, NB)
    got_rows = got.reshape(GROUP * 8, NB)

    def panel_tile(slot):
        return -extra_rows[pl.ds(slot, NB, stride=8), :]

    upper, inverse = factor_and_inverse(panel_tile(6))
    lower = upper.T
    owned, crossing = [], []
    for kk in range(2):
        at_pivot = (2 * layer + kk) * 8 + row == 0
        owned.append(jnp.where(at_pivot, lower, dot_nt(panel_tile(kk), inverse)))
    for kc in range(4):
        at_pivot = kc * 16 + col == 0
        crossing.append(jnp.where(at_pivot, lower, dot_nt(panel_tile(2 + kc), inverse)))
    for kk in range(2):
        for kc in range(4):
            product = dot_nt(owned[kk], crossing[kc])
            out_ref[kk, pl.ds(kc, NB, stride=4), :] = (
                sep_ref[kk, pl.ds(kc, NB, stride=4), :] - product
            )
    own_rows.wait()
    arrived(1, got, got, 8)
    for kk in range(2):
        for kc in range(4):
            update = got_rows[pl.ds(kk * 4 + kc, NB, stride=8), :]
            above = (2 * layer + kk) * 8 + row < kc * 16 + col
            update = jnp.where(above, update.T, update)
            result = out_ref[kk, pl.ds(kc, NB, stride=4), :] - update
            if kc == 0:
                result = jnp.where(col == 0, owned[kk], result)
            out_ref[kk, pl.ds(kc, NB, stride=4), :] = result


def shards(front_pivot, front_border, pivot_live, rows_live, border_block, row_map, separator):
    layer = lax.axis_index("layer")
    own_sep = lax.dynamic_slice_in_dim(separator, layer * 2, 2, 0)
    dma = pltpu.SemaphoreType.DMA
    got, side = pl.pallas_call(
        leaf_kernel,
        out_shape=[
            jax.ShapeDtypeStruct((GROUP, ROWS, NB), f32),
            jax.ShapeDtypeStruct((GROUP, 8, NB), f32),
        ],
        in_specs=[SMEM] * 3 + [VMEM] * 4,
        out_specs=[VMEM, VMEM],
        scratch_shapes=[
            pltpu.VMEM((GROUP, ROWS, NB), f32),
            pltpu.VMEM((GROUP, 8, NB), f32),
            dma((2,)),
            dma((2,)),
            dma((2,)),
        ],
        compiler_params=pltpu.CompilerParams(collective_id=0, has_side_effects=True),
        name="leaf",
    )(
        pivot_live,
        rows_live[0],
        border_block[0],
        row_map[0],
        front_pivot[0],
        front_border[0],
        own_sep[:, :, 0, :],
    )
    places = side[:, 2, :8].astype(jnp.int32).reshape(GROUP * 8)
    gathered, panel = pl.pallas_call(
        collect_kernel,
        out_shape=[
            jax.ShapeDtypeStruct((4 * 1024, NB), f32),
            jax.ShapeDtypeStruct((64, NB), f32),
        ],
        in_specs=[SMEM, VMEM, VMEM],
        out_specs=[VMEM, VMEM],
        name="collect",
    )(places, got.reshape(GROUP * ROWS, NB), side.reshape(GROUP * 8, NB))
    result = pl.pallas_call(
        finish_kernel,
        out_shape=jax.ShapeDtypeStruct((2, 4 * NB, NB), f32),
        in_specs=[VMEM] * 3,
        out_specs=VMEM,
        scratch_shapes=[
            pltpu.VMEM((2, 16, 64, NB), f32),
            pltpu.VMEM((16, 64, NB), f32),
            pltpu.VMEM((16, 64, NB), f32),
            pltpu.VMEM((16, 64, NB), f32),
            pltpu.VMEM((64, NB), f32),
            pltpu.VMEM((3, 64, NB), f32),
            pltpu.VMEM((GROUP, 8, NB), f32),
            pltpu.VMEM((GROUP, 8, NB), f32),
            pltpu.VMEM((GROUP, 8, NB), f32),
            dma((2,)),
            dma((2,)),
            dma((8,)),
            dma((8,)),
            dma((3,)),
            dma((3,)),
            dma((2,)),
            dma((2,)),
            dma((2,)),
        ],
        compiler_params=pltpu.CompilerParams(collective_id=1, has_side_effects=True),
        name="finish",
    )(gathered.reshape(4, 16, 64, NB), panel, own_sep.reshape(2, 4 * NB, NB))
    return result.reshape(2, NB, 4, NB)


def solution(mesh):
    placed = (
        P(("layer", "row", "col"), None, None),
        P(("layer", "row", "col"), None, None),
        P(("layer", "row", "col")),
        P(("layer", "row", "col"), None),
        P(("layer", "row", "col"), None),
        P(("layer", "row", "col"), None, None),
        P(None, "row", None, "col"),
    )
    return jax.shard_map(
        shards,
        mesh=mesh,
        in_specs=placed,
        out_specs=P("layer", "row", None, "col"),
        check_vma=False,
    )
```

time: 167 us -> 111 us (0.66)
  Pallas kernels: 161 us -> 102 us
  local copies, waits for them, and re-layouts: 2.01 us -> 5.72 us
  other arithmetic: 3.13 us -> 1.27 us
    pallas_call x6 -> x3, Pallas kernels: 161 us -> 102 us  [the longest x1 48.2 us: shards(): pl.pallas_call(finish_kernel, out_shape=jax.ShapeDtypeStruct((2, 4 * NB,...]
    unnamed x2 -> x3, local copies, waits for them, and re-layouts: 0.3 us -> 3.46 us
where the time goes in v2:
time: 111 us; the launch traced here: 110 us
  Pallas kernels  102 us (92%)
  local copies, waits for them, and re-layouts  5.72 us (5%)
  other arithmetic  1.27 us (1%)
    pallas_call x1, Pallas kernels, shards(): pl.pallas_call(finish_kernel, out_shape=jax.ShapeDtypeStruct((2, 4 * NB,...  48.2 us
    pallas_call x1, Pallas kernels, shards(): pl.pallas_call(leaf_kernel, out_shape=[jax.ShapeDtypeStruct((GROUP, ROWS,...  47.7 us
    pallas_call x1, Pallas kernels, shards(): pl.pallas_call(collect_kernel, out_shape=[jax.ShapeDtypeStruct((4 * 1024,...  6.48 us
    unnamed x3, local copies, waits for them, and re-layouts  3.46 us

profile of v2, /device:TPU:6, one launch (start us, length us, event | category | flops | bytes accessed | tf_op | source)
XLA Modules:
  0.0 110.0 jit_solution(4250492848405341469)
XLA Ops:
  0.0 0.0 copy-start
  0.0 1.6 %copy-done = f32[8,128,4,128]{3,2,1,0:T(4,128)S(1)} copy-done((f32[8,128,4,128]{3,2,1,0:T(4,128)S(1)}, f32[8,128,4,128]{3,2,1,0:T(4,128)}, u32[]{:S(2)}) %copy-start) | copy-done | bytes 2097176
  1.6 0.7 constant_dynamic-slice_fusion
  3.0 47.7 %leaf.1 = (f32[128,16,128]{2,1,0:T(8,128)}, f32[128,8,128]{2,1,0:T(8,128)}) custom-call(s32[1]{0:T(128)S(6)} %copy.15.live_ref, s32[4]{0:T(128)} %bitcast.22, s32[4]{0:T(128)} %bitcast.23, s32[4,128]{1,0:T(4,128)} %bitcast.21, bf16[256,256]{1,0:T(8,128)(2,1)} %bitcast.20, bf16[512,256]{1,0:T(8,128)(2,1)} %bitcast.19, f32[2,128,128]{2,1,0:T(8,128)} %bitcast.18), custom_call_target="tpu_custom_call" | custom-call | tf_op jit(solution)/shard_map/leaf/pallas_call | solution.py:445
  50.7 1.3 %convert_reduce_fusion = s32[128,8]{1,0:T(8,128)S(1)} fusion(f32[128,8,128]{2,1,0:T(8,128)} %get-tuple-element.9), kind=kLoop, calls=%fused_computation | loop fusion | flops 1024 | bytes 8192 | tf_op jit(solution)/shard_map/convert_element_type | solution.py:471
  52.0 0.7 convert_element_type.8.where_ref
  52.7 6.5 %collect.1 = (f32[4096,128]{1,0:T(8,128)}, f32[64,128]{1,0:T(8,128)}) custom-call(s32[1024]{0:T(1024)} %convert_element_type.8.where_ref, f32[2048,128]{1,0:T(8,128)} %bitcast.16, f32[1024,128]{1,0:T(8,128)} %bitcast.17), custom_call_target="tpu_custom_call" | custom-call | tf_op jit(solution)/shard_map/collect/pallas_call | solution.py:472
  59.1 0.8 constant_dynamic-slice_fusion.1
  60.0 48.2 %finish.1 = f32[2,512,128]{2,1,0:T(8,128)} custom-call(f32[4,16,64,128]{3,2,1,0:T(8,128)} %bitcast.14, f32[64,128]{1,0:T(8,128)} %get-tuple-element.12.panel_ref, f32[2,512,128]{2,1,0:T(8,128)} %bitcast.15), custom_call_target="tpu_custom_call" | custom-call | tf_op jit(solution)/shard_map/finish/pallas_call | solution.py:482
  108.2 1.9 %copy.16 = f32[2,128,4,128]{3,2,1,0:T(4,128)} copy(f32[2,128,4,128]{3,2,1,0:T(4,128)} %bitcast.13) | data formatting | bytes 1048576
Async XLA Ops:
  0.0 1.6 %copy-start = (f32[8,128,4,128]{3,2,1,0:T(4,128)S(1)}, f32[8,128,4,128]{3,2,1,0:T(4,128)}, u32[]{:S(2)}) copy-start(f32[8,128,4,128]{3,2,1,0:T(4,128)} %param.13) | copy-start | bytes 6291460

commit v3 on v2

--- a/solution.py
+++ b/solution.py
@@ -13,6 +13,7 @@
 ROWS = 16
 VMEM = pl.BlockSpec(memory_space=pltpu.VMEM)
 SMEM = pl.BlockSpec(memory_space=pltpu.SMEM)
+ANY = pl.BlockSpec(memory_space=pl.ANY)
 
 
 def dot_nt(a, b):
@@ -120,9 +121,13 @@
 
 def leaf_kernel(
     live_ref, rows_ref, block_ref, map_ref, pivot_ref, border_ref, sep_ref,
-    got_ref, side_ref, out, early, send_sem, recv_sem, own_sem,
+    got_ref, side_ref, out, early, column, send_sem, recv_sem, own_sem, column_sem,
 ):
     peers = Peers()
+    fetch = pltpu.make_async_copy(
+        sep_ref.at[pl.ds(peers.layer * 2, 2), :, 0, :], column, column_sem
+    )
+    fetch.start()
     barrier = pltpu.get_barrier_semaphore()
 
     def greet(target, place):
@@ -156,8 +161,6 @@
         where_row = jnp.where(lane == s, row_at, where_row)
         where_row = jnp.where(lane == 4 + s, col_at, where_row)
     early_rows = early.reshape(GROUP * 8, NB)
-    for k in range(2):
-        early_rows[pl.ds(k, NB, stride=8), :] = sep_ref[k]
     early_rows[pl.ds(2, NB, stride=8), :] = where_row.astype(f32)
 
     live = live_ref[0]
@@ -170,6 +173,9 @@
     )
     first = factor_and_inverse(front[:NB, :NB])[1]
 
+    fetch.wait()
+    for k in range(2):
+        early_rows[pl.ds(k, NB, stride=8), :] = column[k]
     pl.semaphore_wait(barrier, GROUP - 1)
     own_side = pltpu.make_async_copy(
         early.at[peers.me, pl.ds(0, 3)], side_ref.at[peers.me, pl.ds(0, 3)], own_sem.at[0]
@@ -246,7 +252,11 @@
         everything.wait_recv()
 
 
-def collect_kernel(where_ref, got_ref, side_ref, out_ref, panel_ref):
+def collect_kernel(got_ref, side_ref, out_ref, panel_ref, where_at, column, sems):
+    get_places = pltpu.make_async_copy(side_ref.at[:, :, 2, :], where_at, sems.at[0])
+    get_column = pltpu.make_async_copy(side_ref.at[:, 0], column, sems.at[1])
+    get_places.start()
+    get_column.start()
     core_here = lax.rem(lax.axis_index("layer"), 2)
     low = lax.rem(lax.axis_index("col"), 2)
 
@@ -255,10 +265,13 @@
         return carry
 
     lax.fori_loop(0, 32, clear, 0)
+    get_places.wait()
+    get_column.wait()
 
     def add(leaf, carry):
-        rows = [where_ref[leaf * 8 + g] for g in range(4)]
-        cols = [where_ref[leaf * 8 + 4 + g] for g in range(4)]
+        high, low_part = leaf // 8, lax.rem(leaf, 8)
+        rows = [where_at[high, low_part, g].astype(jnp.int32) for g in range(4)]
+        cols = [where_at[high, low_part, 4 + g].astype(jnp.int32) for g in range(4)]
         places, values = [], []
         slot = 0
         for s in range(4):
@@ -281,16 +294,27 @@
         high, core = layer // 2, layer % 2
         at = core * 1024 + high * 512 + row * 64 + kk * 4
         mine = jnp.where((low == 0) & (core_here == core), 1.0, 0.0)
-        given = side_ref[pl.ds((high * 64 + row * 8) * 8 + kk, 1), :]
+        given = column[high * 8 + row, kk : kk + 1, :]
         panel_ref[pl.ds(block, 1), :] = out_ref[pl.ds(at, 1), :] - given * mine
 
 
 def finish_kernel(
-    src_ref, panel_ref, sep_ref, out_ref, near, cross, passing, total, joined, others, fan,
+    src_ref, panel_ref, sep_ref, out_ref, held, corner, near, cross, passing, total, joined, others, fan,
     got, extra, twin_send, twin_recv, cross_send, cross_recv, panel_send, panel_recv,
-    send_sem, recv_sem, own_sem,
+    send_sem, recv_sem, own_sem, load_sem,
 ):
     peers = Peers()
+    loads = [
+        pltpu.make_async_copy(
+            src_ref.at[q * 2 + peers.core], held.at[q], load_sem.at[q]
+        )
+        for q in range(2)
+    ]
+    loads.append(
+        pltpu.make_async_copy(sep_ref.at[pl.ds(peers.layer * 2, 2)], corner, load_sem.at[2])
+    )
+    for load in loads:
+        load.start()
     layer, row, col = peers.layer, peers.row, peers.col
     core, low, me = peers.core, peers.low, peers.me
     twin = (layer + 1 - 2 * core, row, col)
@@ -320,11 +344,13 @@
     for copy in (*panels, onward, kept):
         copy.start()
 
+    for load in loads:
+        load.wait()
     onward.wait()
     across = []
     for dz in range(8):
         piece = pl.ds(pl.multiple_of(peers.depths[dz] * 8, 8), 8)
-        passing[:, piece, :] = src_ref[(1 - low) * 2 + core, :, piece, :] + near[0, :, piece, :]
+        passing[:, piece, :] = held[1 - low, :, piece, :] + near[0, :, piece, :]
         across.append(
             remote(
                 passing.at[:, piece],
@@ -334,8 +360,7 @@
                 beside,
             )
         )
-        if dz < 2:
-            across[dz].start()
+        across[dz].start()
 
     for copy in panels:
         copy.wait()
@@ -368,15 +393,13 @@
         ).start()
 
     peers.visit(send_extra)
-    for dz in range(2, 8):
-        across[dz].start()
     kept.wait()
     own_rows = None
     for dz in range(8):
         piece = pl.ds(pl.multiple_of(peers.depths[dz] * 8, 8), 8)
         across[dz].wait()
         total[:, piece, :] = (
-            src_ref[low * 2 + core, :, piece, :] + near[1, :, piece, :] + cross[:, piece, :]
+            held[low, :, piece, :] + near[1, :, piece, :] + cross[:, piece, :]
         )
         if dz == 0:
             own_rows = pltpu.make_async_copy(
@@ -423,7 +446,7 @@
         for kc in range(4):
             product = dot_nt(owned[kk], crossing[kc])
             out_ref[kk, pl.ds(kc, NB, stride=4), :] = (
-                sep_ref[kk, pl.ds(kc, NB, stride=4), :] - product
+                corner[kk, pl.ds(kc, NB, stride=4), :] - product
             )
     own_rows.wait()
     arrived(1, got, got, 8)
@@ -439,8 +462,6 @@
 
 
 def shards(front_pivot, front_border, pivot_live, rows_live, border_block, row_map, separator):
-    layer = lax.axis_index("layer")
-    own_sep = lax.dynamic_slice_in_dim(separator, layer * 2, 2, 0)
     dma = pltpu.SemaphoreType.DMA
     got, side = pl.pallas_call(
         leaf_kernel,
@@ -448,14 +469,16 @@
             jax.ShapeDtypeStruct((GROUP, ROWS, NB), f32),
             jax.ShapeDtypeStruct((GROUP, 8, NB), f32),
         ],
-        in_specs=[SMEM] * 3 + [VMEM] * 4,
+        in_specs=[SMEM] * 3 + [VMEM] * 3 + [ANY],
         out_specs=[VMEM, VMEM],
         scratch_shapes=[
             pltpu.VMEM((GROUP, ROWS, NB), f32),
             pltpu.VMEM((GROUP, 8, NB), f32),
-            dma((2,)),
-            dma((2,)),
-            dma((2,)),
+            pltpu.VMEM((2, NB, NB), f32),
+            dma((2,)),
+            dma((2,)),
+            dma((2,)),
+            dma,
         ],
         compiler_params=pltpu.CompilerParams(collective_id=0, has_side_effects=True),
         name="leaf",
@@ -466,25 +489,27 @@
         row_map[0],
         front_pivot[0],
         front_border[0],
-        own_sep[:, :, 0, :],
-    )
-    places = side[:, 2, :8].astype(jnp.int32).reshape(GROUP * 8)
+        separator,
+    )
     gathered, panel = pl.pallas_call(
         collect_kernel,
         out_shape=[
             jax.ShapeDtypeStruct((4 * 1024, NB), f32),
             jax.ShapeDtypeStruct((64, NB), f32),
         ],
-        in_specs=[SMEM, VMEM, VMEM],
+        in_specs=[VMEM, ANY],
         out_specs=[VMEM, VMEM],
+        scratch_shapes=[pltpu.SMEM((16, 8, NB), f32), pltpu.VMEM((16, 8, NB), f32), dma((2,))],
         name="collect",
-    )(places, got.reshape(GROUP * ROWS, NB), side.reshape(GROUP * 8, NB))
+    )(got.reshape(GROUP * ROWS, NB), side.reshape(16, 8, 8, NB))
     result = pl.pallas_call(
         finish_kernel,
         out_shape=jax.ShapeDtypeStruct((2, 4 * NB, NB), f32),
-        in_specs=[VMEM] * 3,
+        in_specs=[ANY, VMEM, ANY],
         out_specs=VMEM,
         scratch_shapes=[
+            pltpu.VMEM((2, 16, 64, NB), f32),
+            pltpu.VMEM((2, 4 * NB, NB), f32),
             pltpu.VMEM((2, 16, 64, NB), f32),
             pltpu.VMEM((16, 64, NB), f32),
             pltpu.VMEM((16, 64, NB), f32),
@@ -503,10 +528,11 @@
             dma((2,)),
             dma((2,)),
             dma((2,)),
+            dma((3,)),
         ],
         compiler_params=pltpu.CompilerParams(collective_id=1, has_side_effects=True),
         name="finish",
-    )(gathered.reshape(4, 16, 64, NB), panel, own_sep.reshape(2, 4 * NB, NB))
+    )(gathered.reshape(4, 16, 64, NB), panel, separator.reshape(8, 4 * NB, NB))
     return result.reshape(2, NB, 4, NB)
 
 

time: 111 us -> 108 us (0.973)
  local copies, waits for them, and re-layouts: 5.72 us -> 1.87 us
  Pallas kernels: 102 us -> 105 us
  other arithmetic: 1.27 us -> 0 us
    pallas_call x1, Pallas kernels: 6.48 us -> 9.91 us  [shards(): pl.pallas_call(collect_kernel, out_shape=[jax.ShapeDtypeStruct((4 * 1024,...]
    unnamed x3 -> x1, local copies, waits for them, and re-layouts: 3.46 us -> 1.87 us
    convert_element_type x1 -> x0, other arithmetic: 1.27 us -> none  [shards(): places = side[:, 2, :8].astype(jnp.int32).reshape(GROUP * 8)]
    pallas_call x1, Pallas kernels: 48.2 us -> 47 us  [shards(): pl.pallas_call(finish_kernel, out_shape=jax.ShapeDtypeStruct((2, 4 * NB,...]
where the time goes in v3:
time: 108 us; the launch traced here: 107 us
  Pallas kernels  105 us (97%)
  local copies, waits for them, and re-layouts  1.87 us (2%)
    pallas_call x1, Pallas kernels, shards(): pl.pallas_call(leaf_kernel, out_shape=[jax.ShapeDtypeStruct((GROUP, ROWS,...  47.7 us
    pallas_call x1, Pallas kernels, shards(): pl.pallas_call(finish_kernel, out_shape=jax.ShapeDtypeStruct((2, 4 * NB,...  47 us
    pallas_call x1, Pallas kernels, shards(): pl.pallas_call(collect_kernel, out_shape=[jax.ShapeDtypeStruct((4 * 1024,...  9.91 us

profile of v3, /device:TPU:6, one launch (start us, length us, event | category | flops | bytes accessed | tf_op | source)
XLA Modules:
  0.0 107.2 jit_solution(18130106547332109933)
XLA Ops:
  0.7 47.7 %leaf.1 = (f32[128,16,128]{2,1,0:T(8,128)}, f32[128,8,128]{2,1,0:T(8,128)}) custom-call(s32[1]{0:T(128)S(6)} %copy.9.live_ref, s32[4]{0:T(128)} %bitcast.18, s32[4]{0:T(128)} %bitcast.19, s32[4,128]{1,0:T(4,128)} %bitcast.17, bf16[256,256]{1,0:T(8,128)(2,1)} %bitcast.16, bf16[512,256]{1,0:T(8,128)(2,1)} %bitcast.15, f32[8,128,4,128]{3,2,1,0:T(4,128)} %sep_ref.1), custom_call_target="tpu_custom_call" | custom-call | tf_op jit(solution)/shard_map/leaf/pallas_call | solution.py:466
  48.3 9.9 %collect.1 = (f32[4096,128]{1,0:T(8,128)}, f32[64,128]{1,0:T(8,128)}) custom-call(f32[2048,128]{1,0:T(8,128)} %bitcast.13, f32[16,8,8,128]{3,2,1,0:T(8,128)} %bitcast.14), custom_call_target="tpu_custom_call" | custom-call | tf_op jit(solution)/shard_map/collect/pallas_call | solution.py:494
  58.3 47.0 %finish.1 = f32[2,512,128]{2,1,0:T(8,128)} custom-call(f32[4,16,64,128]{3,2,1,0:T(8,128)} %bitcast.11, f32[64,128]{1,0:T(8,128)} %get-tuple-element.12.panel_ref, f32[8,512,128]{2,1,0:T(8,128)} %bitcast.10), custom_call_target="tpu_custom_call" | custom-call | tf_op jit(solution)/shard_map/finish/pallas_call | solution.py:505
  105.3 1.9 %copy.10 = f32[2,128,4,128]{3,2,1,0:T(4,128)} copy(f32[2,128,4,128]{3,2,1,0:T(4,128)} %bitcast.12) | data formatting | bytes 1048576

commit v4 on v3

--- a/solution.py
+++ b/solution.py
@@ -252,8 +252,8 @@
         everything.wait_recv()
 
 
-def collect_kernel(got_ref, side_ref, out_ref, panel_ref, where_at, column, sems):
-    get_places = pltpu.make_async_copy(side_ref.at[:, :, 2, :], where_at, sems.at[0])
+def collect_kernel(got_ref, side_ref, out_ref, panel_ref, where_at, given_at, whole, column, sems):
+    get_places = pltpu.make_async_copy(side_ref.at[:, :, 2, :], given_at, sems.at[0])
     get_column = pltpu.make_async_copy(side_ref.at[:, 0], column, sems.at[1])
     get_places.start()
     get_column.start()
@@ -264,14 +264,18 @@
         out_ref[pl.ds(pl.multiple_of(i * 128, 128), 128), :] = jnp.zeros((128, NB), f32)
         return carry
 
+    get_places.wait()
+    whole[...] = given_at[...].astype(jnp.int32)
+    to_scalars = pltpu.make_async_copy(whole, where_at, sems.at[2])
+    to_scalars.start()
     lax.fori_loop(0, 32, clear, 0)
-    get_places.wait()
+    to_scalars.wait()
     get_column.wait()
 
     def add(leaf, carry):
         high, low_part = leaf // 8, lax.rem(leaf, 8)
-        rows = [where_at[high, low_part, g].astype(jnp.int32) for g in range(4)]
-        cols = [where_at[high, low_part, 4 + g].astype(jnp.int32) for g in range(4)]
+        rows = [where_at[high, low_part, g] for g in range(4)]
+        cols = [where_at[high, low_part, 4 + g] for g in range(4)]
         places, values = [], []
         slot = 0
         for s in range(4):
@@ -499,7 +503,13 @@
         ],
         in_specs=[VMEM, ANY],
         out_specs=[VMEM, VMEM],
-        scratch_shapes=[pltpu.SMEM((16, 8, NB), f32), pltpu.VMEM((16, 8, NB), f32), dma((2,))],
+        scratch_shapes=[
+            pltpu.SMEM((16, 8, NB), jnp.int32),
+            pltpu.VMEM((16, 8, NB), f32),
+            pltpu.VMEM((16, 8, NB), jnp.int32),
+            pltpu.VMEM((16, 8, NB), f32),
+            dma((3,)),
+        ],
         name="collect",
     )(got.reshape(GROUP * ROWS, NB), side.reshape(16, 8, 8, NB))
     result = pl.pallas_call(

time: 108 us -> 107 us (level)
  no operation moved by 1% of the time
where the time goes in v4:
time: 107 us
  Pallas kernels  104 us (97%)
  local copies, waits for them, and re-layouts  1.87 us (2%)
    pallas_call x1, Pallas kernels, shards(): pl.pallas_call(leaf_kernel, out_shape=[jax.ShapeDtypeStruct((GROUP, ROWS,...  47.7 us
    pallas_call x1, Pallas kernels, shards(): pl.pallas_call(finish_kernel, out_shape=jax.ShapeDtypeStruct((2, 4 * NB,...  47 us
    pallas_call x1, Pallas kernels, shards(): pl.pallas_call(collect_kernel, out_shape=[jax.ShapeDtypeStruct((4 * 1024,...  9.57 us

profile of v4, /device:TPU:6, one launch (start us, length us, event | category | flops | bytes accessed | tf_op | source)
XLA Modules:
  0.0 106.8 jit_solution(17959065403011693331)
XLA Ops:
  0.7 47.7 %leaf.1 = (f32[128,16,128]{2,1,0:T(8,128)}, f32[128,8,128]{2,1,0:T(8,128)}) custom-call(s32[1]{0:T(128)S(6)} %copy.9.live_ref, s32[4]{0:T(128)} %bitcast.18, s32[4]{0:T(128)} %bitcast.19, s32[4,128]{1,0:T(4,128)} %bitcast.17, bf16[256,256]{1,0:T(8,128)(2,1)} %bitcast.16, bf16[512,256]{1,0:T(8,128)(2,1)} %bitcast.15, f32[8,128,4,128]{3,2,1,0:T(4,128)} %sep_ref.1), custom_call_target="tpu_custom_call" | custom-call | tf_op jit(solution)/shard_map/leaf/pallas_call | solution.py:470
  48.3 9.6 %collect.1 = (f32[4096,128]{1,0:T(8,128)}, f32[64,128]{1,0:T(8,128)}) custom-call(f32[2048,128]{1,0:T(8,128)} %bitcast.13, f32[16,8,8,128]{3,2,1,0:T(8,128)} %bitcast.14), custom_call_target="tpu_custom_call" | custom-call | tf_op jit(solution)/shard_map/collect/pallas_call | solution.py:498
  57.9 47.0 %finish.1 = f32[2,512,128]{2,1,0:T(8,128)} custom-call(f32[4,16,64,128]{3,2,1,0:T(8,128)} %bitcast.11, f32[64,128]{1,0:T(8,128)} %get-tuple-element.12.panel_ref, f32[8,512,128]{2,1,0:T(8,128)} %bitcast.10), custom_call_target="tpu_custom_call" | custom-call | tf_op jit(solution)/shard_map/finish/pallas_call | solution.py:515
  105.0 1.9 %copy.10 = f32[2,128,4,128]{3,2,1,0:T(4,128)} copy(f32[2,128,4,128]{3,2,1,0:T(4,128)} %bitcast.12) | data formatting | bytes 1048576
